TPU v7x, 32 devices: a whole 2x2x4 slice. The times are simulated.
32 devices in a mesh: seq: 8 (over z, y), tensor: 4 (over x, core).
Axes of the slice: x: 2, y: 2, z: 4, core: 2. Of those that a mesh axis runs over, the one named last changes fastest.
Arguments:
- queries: bfloat16 [2048, 8192], P('seq', 'tensor'), may hold values from -4 to 4, as said below
- keys: bfloat16 [2048, 1024], P('seq', 'tensor'), may hold values from -96 to 96, as said below
- values: bfloat16 [2048, 1024], P('seq', 'tensor'), may hold values from -6 to 6
- block_pos: int32 [16], replicated, may hold values from 0 to 15, each once
Outputs:
- attended: bfloat16 [2048, 8192], P('seq')
Inputs may be any that keep to these rules, and one draw needn't show every extreme that they name: block_pos is a permutation of 0 to 15. real-valued queries. real-valued keys.
All inputs are finite; a program needn't handle non-finite values.
Results may differ from a plain program's by a relative error of at most 0.004.
Values may be sent and summed in bfloat16 or wider, within the bound.
A program may use at most 64 MiB of HBM per device.

v0:
```python
import math

import jax
import jax.numpy as jnp
from jax import lax
from jax.sharding import PartitionSpec as P

QUERY_HEADS = 64
KEY_VALUE_HEADS = 8
HEAD_WIDTH = 128
VISIBLE_SHARDS = 4


def from_behind(block, axis, distance):
    devices = range(lax.axis_size(axis))
    route = [((i - distance) % len(devices), i) for i in devices]
    return lax.ppermute(block, axis, route)


def shard_positions(block_pos, shard, block_len):
    pair = lax.dynamic_slice_in_dim(block_pos, 2 * shard, 2, 0)
    offsets = jnp.arange(block_len, dtype=jnp.int32)
    return (pair[:, None] * block_len + offsets[None, :]).reshape(-1)


def attend(query_rows, q_pos, key_gathered, value_gathered, key_pos):
    rows = query_rows.shape[0]
    groups = key_gathered.shape[1]
    group_factor = QUERY_HEADS // KEY_VALUE_HEADS
    q_heads = query_rows.reshape(rows, groups, group_factor, HEAD_WIDTH)
    scores = jnp.einsum("qgrd,kgd->grqk", q_heads, key_gathered, preferred_element_type=jnp.float32)
    scores = scores * (1.0 / math.sqrt(HEAD_WIDTH))
    allowed = key_pos[None, :] <= q_pos[:, None]
    scores = jnp.where(allowed[None, None], scores, -1e30)
    top = jnp.max(scores, axis=-1, keepdims=True)
    weights = jnp.exp(scores - top)
    total = jnp.sum(weights, axis=-1)
    rounded = weights.astype(jnp.bfloat16)
    mixed = jnp.einsum(
        "grqk,kgd->qgrd", rounded, value_gathered, preferred_element_type=jnp.float32
    )
    mixed = mixed / jnp.transpose(total, (2, 0, 1))[..., None]
    return mixed.reshape(rows, groups * group_factor * HEAD_WIDTH).astype(jnp.bfloat16)


def body(queries, keys, values, block_pos):
    tok_rows = queries.shape[0]
    block_len = tok_rows // 2
    groups = keys.shape[1] // HEAD_WIDTH
    shard = lax.axis_index("seq")
    count = lax.axis_size("seq")
    stacked = jnp.stack([keys, values])
    pieces = [stacked]
    current = stacked
    for back in range(1, VISIBLE_SHARDS):
        current = from_behind(current, "seq", 1)
        pieces.append(current)
    key_gathered = jnp.concatenate([piece[0] for piece in pieces], 0).reshape(
        VISIBLE_SHARDS * tok_rows, groups, HEAD_WIDTH
    )
    value_gathered = jnp.concatenate([piece[1] for piece in pieces], 0).reshape(
        VISIBLE_SHARDS * tok_rows, groups, HEAD_WIDTH
    )
    key_pos = jnp.concatenate(
        [
            shard_positions(block_pos, (shard - back) % count, block_len)
            for back in range(VISIBLE_SHARDS)
        ],
        0,
    )
    q_pos = shard_positions(block_pos, shard, block_len)
    halves = []
    for half in range(2):
        q_part = queries[half * block_len : (half + 1) * block_len]
        pos_part = q_pos[half * block_len : (half + 1) * block_len]
        local = attend(q_part, pos_part, key_gathered, value_gathered, key_pos)
        halves.append(lax.all_gather(local, "tensor", axis=1, tiled=True))
    return jnp.concatenate(halves, 0)


def solution(mesh):
    placed = (P("seq", "tensor"), P("seq", "tensor"), P("seq", "tensor"), P())
    return jax.shard_map(
        body, mesh=mesh, in_specs=placed, out_specs=P("seq", None), check_vma=False
    )
```

profile of v0, /device:TPU:0, one launch (start us, length us, event | category | flops | bytes accessed | tf_op | source)
XLA Modules:
  0.0 102.2 jit_solution(1030988277564516786)
XLA Ops:
  6.5 0.0 all-gather.5.cloned.1.call-start
  6.5 1.0 copy.14
  7.5 1.0 copy.13
  8.6 3.0 %collective-permute-start = (bf16[2,256,256]{1,2,0:T(8,128)(2,1)S(1)}, bf16[2,256,256]{1,2,0:T(8,128)(2,1)S(1)}, u32[]{:S(2)}, u32[]{:S(2)}) collective-permute-start(bf16[2,256,256]{1,2,0:T(8,128)(2,1)S(1)} %pad_maximum_fusion.1), channel_id=1, source_target_pairs={{28,0},{0,4},{4,8},{8,12},{12,16},{16,20},{20,24},{24,28},{29,1},{... | collective-permute-start | bytes 786440 | tf_op jit(solution)/shard_map/ppermute | solution.py:17
  11.6 0.9 dynamic-slice_multiply_fusion.4
  12.6 0.1 iota_add_fusion
  12.6 1.3 %fusion.32 = (bf16[128,2048]{1,0:T(8,128)(2,1)S(1)}, bf16[128,2048]{1,0:T(8,128)(2,1)S(1)}) fusion(bf16[256,2048]{1,0:T(8,128)(2,1)} %param.4), kind=kLoop, calls=%fused_computation.47 | loop fusion | bytes 2097152 | tf_op jit(solution)/shard_map/slice | solution.py:74
  13.9 0.1 add_bitcast_fusion.2
  14.0 0.1 add_bitcast_fusion
  14.0 6.9 %collective-permute-done = bf16[2,256,256]{1,2,0:T(8,128)(2,1)S(1)} collective-permute-done((bf16[2,256,256]{1,2,0:T(8,128)(2,1)S(1)}, bf16[2,256,256]{1,2,0:T(8,128)(2,1)S(1)}, u32[]{:S(2)}, u32[]{:S(2)}) %collective-permute-start) | collective-permute-done | bytes 262176 | tf_op jit(solution)/shard_map/ppermute | solution.py:17
  21.0 0.0 collective-permute-start.1
  21.0 0.1 copy.17
  21.1 0.3 copy.36
  21.4 0.2 broadcast_compare_fusion.1
  21.6 9.5 %collective-permute-done.1 = bf16[2,256,256]{1,2,0:T(8,128)(2,1)S(1)} collective-permute-done((bf16[2,256,256]{1,2,0:T(8,128)(2,1)S(1)}, bf16[2,256,256]{1,2,0:T(8,128)(2,1)S(1)}, u32[]{:S(2)}, u32[]{:S(2)}) %collective-permute-start.1) | collective-permute-done | bytes 262176 | tf_op jit(solution)/shard_map/ppermute | solution.py:17
  31.2 0.0 collective-permute-start.2
  31.2 0.1 copy.18
  31.3 0.1 copy.19
  31.5 9.0 %collective-permute-done.2 = bf16[2,256,256]{1,2,0:T(8,128)(2,1)S(1)} collective-permute-done((bf16[2,256,256]{1,2,0:T(8,128)(2,1)S(1)}, bf16[2,256,256]{1,2,0:T(8,128)(2,1)S(1)}, u32[]{:S(2)}, u32[]{:S(2)}) %collective-permute-start.2) | collective-permute-done | bytes 262176 | tf_op jit(solution)/shard_map/ppermute | solution.py:17
  40.5 0.1 copy.20
  40.6 1.3 %fusion.5 = (f32[2,8,128]{2,1,0:T(8,128)S(1)}, f32[2,1024,128,8]{2,1,3,0:T(8,128)S(1)}) fusion(pred[128,1024]{0,1:T(8,128)(4,1)S(1)} %get-tuple-element.14, bf16[128,2,8,128]{0,3,2,1:T(8,128)(2,1)S(1)} %bitcast.82, bf16[256,2,128]{2,0,1:T(8,128)(2,1)S(1)} %copy.20, bf16[256,2,128]{2,0,1:T(8,128)(2,1)S(1)} %copy.19, bf16[256,2,128]{2,0,1:T(8,128)(2,1)S(1)} %copy.18, ...), kind=kOutput, calls=%fused_computation.9 | convolution fusion | flops 545257472 | bytes 9576448 | tf_op jit(solution)/shard_map/qgrd,kgd->grqk/dot_general | solution.py:31
  41.9 1.7 %fusion.2 = f32[2,8,128]{2,1,0:T(8,128)S(1)} fusion(f32[2,1024,128,8]{2,1,3,0:T(8,128)S(1)} %get-tuple-element.23, f32[2,8,128]{2,1,0:T(8,128)S(1)} %get-tuple-element.22, pred[128,1024]{0,1:T(8,128)(4,1)S(1)} %get-tuple-element.14), kind=kLoop, calls=%fused_computation.6 | loop fusion | flops 8386560 | bytes 8536064 | tf_op jit(solution)/shard_map/reduce_sum | solution.py:37
  43.7 2.2 %divide_convert_fusion = bf16[128,2,8,128]{0,3,2,1:T(8,128)(2,1)S(1)} fusion(f32[2,1024,128,8]{2,1,3,0:T(8,128)S(1)} %get-tuple-element.23, f32[2,8,128]{2,1,0:T(8,128)S(1)} %get-tuple-element.22, pred[128,1024]{0,1:T(8,128)(4,1)S(1)} %get-tuple-element.14, f32[128,2,8]{0,2,1:T(8,128)S(1)} %bitcast.99, bf16[256,2,128]{0,2,1:T(8,128)(2,1)S(1)} %bitcast.96, ...), kind=kOutput, calls=%fused_computation.17 | convolution fusion | flops 547880960 | bytes 9584640 | tf_op jit(solution)/shard_map/grqk,kgd->qgrd/dot_general | solution.py:39
  45.8 1.0 copy.28
  46.8 0.0 all-gather.5.cloned.1.call-update
  46.9 0.2 all-gather.3.cloned.1.call-start
  47.1 0.3 copy.35
  47.4 1.3 %fusion.4 = (f32[2,8,128]{2,1,0:T(8,128)S(1)}, f32[2,1024,128,8]{2,1,3,0:T(8,128)S(1)}) fusion(pred[128,1024]{0,1:T(8,128)(4,1)S(1)} %get-tuple-element.13, bf16[128,2,8,128]{0,3,2,1:T(8,128)(2,1)S(1)} %bitcast.83, bf16[256,2,128]{2,0,1:T(8,128)(2,1)S(1)} %copy.20, bf16[256,2,128]{2,0,1:T(8,128)(2,1)S(1)} %copy.19, bf16[256,2,128]{2,0,1:T(8,128)(2,1)S(1)} %copy.18, ...), kind=kOutput, calls=%fused_computation.8 | convolution fusion | flops 545257472 | bytes 9576448 | tf_op jit(solution)/shard_map/qgrd,kgd->grqk/dot_general | solution.py:31
  48.7 1.7 %fusion = f32[2,8,128]{2,1,0:T(8,128)S(1)} fusion(f32[2,1024,128,8]{2,1,3,0:T(8,128)S(1)} %get-tuple-element.25, f32[2,8,128]{2,1,0:T(8,128)S(1)} %get-tuple-element.24, pred[128,1024]{0,1:T(8,128)(4,1)S(1)} %get-tuple-element.13), kind=kLoop, calls=%fused_computation.4 | loop fusion | flops 8386560 | bytes 8536064 | tf_op jit(solution)/shard_map/reduce_sum | solution.py:37
  50.4 2.2 %divide_convert_fusion.1 = bf16[128,2,8,128]{0,3,2,1:T(8,128)(2,1)S(1)} fusion(f32[2,1024,128,8]{2,1,3,0:T(8,128)S(1)} %get-tuple-element.25, f32[2,8,128]{2,1,0:T(8,128)S(1)} %get-tuple-element.24, pred[128,1024]{0,1:T(8,128)(4,1)S(1)} %get-tuple-element.13, f32[128,2,8]{0,2,1:T(8,128)S(1)} %bitcast.98, bf16[256,2,128]{0,2,1:T(8,128)(2,1)S(1)} %bitcast.97, ...), kind=kOutput, calls=%fused_computation.18 | convolution fusion | flops 547880960 | bytes 9584640 | tf_op jit(solution)/shard_map/grqk,kgd->qgrd/dot_general | solution.py:39
  52.6 1.0 %copy.24 = bf16[128,2048]{1,0:T(8,128)(2,1)} copy(bf16[128,2048]{0,1:T(8,128)(2,1)S(1)} %bitcast.84) | data formatting | bytes 1048576 | tf_op jit(solution)/shard_map/convert_element_type | solution.py:43
  53.6 0.0 all-gather.3.cloned.1.call-update
  53.7 12.9 %all-gather.5.cloned.1.call-done = bf16[128,8192]{1,0:T(8,128)(2,1)} async-done(((bf16[128,2048]{1,0:T(8,128)(2,1)}), bf16[128,8192]{1,0:T(8,128)(2,1)}) %all-gather.5.cloned.1.call-update) | async-done | bytes 2097168 | tf_op jit(solution)/shard_map/all_gather | solution.py:77
  66.5 24.2 %all-gather.3.cloned.1.call-done = bf16[128,8192]{1,0:T(8,128)(2,1)} async-done(((bf16[128,2048]{1,0:T(8,128)(2,1)}), bf16[128,8192]{1,0:T(8,128)(2,1)}) %all-gather.3.cloned.1.call-update) | async-done | bytes 2097168 | tf_op jit(solution)/shard_map/all_gather | solution.py:77
  90.7 4.7 %pad_maximum_fusion = bf16[256,8192]{1,0:T(8,128)(2,1)} fusion(bf16[128,8192]{1,0:T(8,128)(2,1)} %all-gather.5.cloned.1.call-done, bf16[128,8192]{1,0:T(8,128)(2,1)} %all-gather.3.cloned.1.call-done), kind=kLoop, calls=%fused_computation.10 | loop fusion | flops 8388608 | bytes 8388608 | tf_op jit(solution)/shard_map/concatenate | solution.py:78
  (6 shorter events, 0.1 us)
Async XLA Ops:
  6.5 60.0 %all-gather.5.cloned.1.call-start = ((), (), s32[]{:S(2)}) async-start(), calls=%async_computation.1 | async-start | bytes 2621440 | tf_op jit(solution)/shard_map/all_gather | solution.py:77
  8.6 12.4 %collective-permute-start = (bf16[2,256,256]{1,2,0:T(8,128)(2,1)S(1)}, bf16[2,256,256]{1,2,0:T(8,128)(2,1)S(1)}, u32[]{:S(2)}, u32[]{:S(2)}) collective-permute-start(bf16[2,256,256]{1,2,0:T(8,128)(2,1)S(1)} %pad_maximum_fusion.1), channel_id=1, source_target_pairs={{28,0},{0,4},{4,8},{8,12},{12,16},{16,20},{20,24},{24,28},{29,1},{... | collective-permute-start | bytes 786440 | tf_op jit(solution)/shard_map/ppermute | solution.py:17
  21.0 10.2 %collective-permute-start.1 = (bf16[2,256,256]{1,2,0:T(8,128)(2,1)S(1)}, bf16[2,256,256]{1,2,0:T(8,128)(2,1)S(1)}, u32[]{:S(2)}, u32[]{:S(2)}) collective-permute-start(bf16[2,256,256]{1,2,0:T(8,128)(2,1)S(1)} %collective-permute-done), channel_id=1, source_target_pairs={{28,0},{0,4},{4,8},{8,12},{12,16},{16,20},{20,24},{24,28},{29,1},{... | collective-permute-start | bytes 786440 | tf_op jit(solution)/shard_map/ppermute | solution.py:17
  31.2 9.3 %collective-permute-start.2 = (bf16[2,256,256]{1,2,0:T(8,128)(2,1)S(1)}, bf16[2,256,256]{1,2,0:T(8,128)(2,1)S(1)}, u32[]{:S(2)}, u32[]{:S(2)}) collective-permute-start(bf16[2,256,256]{1,2,0:T(8,128)(2,1)S(1)} %collective-permute-done.1), channel_id=1, source_target_pairs={{28,0},{0,4},{4,8},{8,12},{12,16},{16,20},{20,24},{24,28},{29,1},{... | collective-permute-start | bytes 786440 | tf_op jit(solution)/shard_map/ppermute | solution.py:17
  46.9 43.8 %all-gather.3.cloned.1.call-start = ((), (), s32[]{:S(2)}) async-start(), calls=%async_computation | async-start | bytes 2621440 | tf_op jit(solution)/shard_map/all_gather | solution.py:77
Sparse Core Ops, SparseCore 0:
  47.0 19.4 all-gather.4
  68.1 22.5 all-gather.2
where the time goes:
time: 102 us
  waiting for transfers between devices  62.5 us (61%)
  between operations  13.5 us (13%)
  other arithmetic  9.54 us (9%)
  matrix products  6.94 us (7%)
  local copies, waits for them, and re-layouts  6.4 us (6%)
  starting transfers between devices  3.28 us (3%)
    all_gather x2, waiting for transfers between devices, body(): halves.append(lax.all_gather(local, 'tensor', axis=1, tiled=True))  37 us
    ppermute x3, waiting for transfers between devices, from_behind(): return lax.ppermute(block, axis, route)  25.5 us
    concatenate x1, other arithmetic, body(): return jnp.concatenate(halves, 0)  4.67 us
    dot_general x2, matrix products, attend(): jnp.einsum('grqk,kgd->qgrd', rounded, value_gathered, preferred_element_t...  4.34 us
    reduce_sum x2, other arithmetic, attend(): total = jnp.sum(weights, axis=-1)  3.49 us
    ppermute x3, starting transfers between devices, from_behind(): return lax.ppermute(block, axis, route)  3.05 us
    dot_general x2, matrix products, attend(): jnp.einsum('qgrd,kgd->grqk', q_heads, key_gathered, preferred_element_typ...  2.6 us
    unnamed x4, local copies, waits for them, and re-layouts  2.55 us
  transfers between devices with their start and end apart: 5, of which 5 were waited for; matrix products, arithmetic and copies ran while one was open for 10% of the time, Pallas kernels for 0%

commit v1 on v0

v1 whole, which is shorter than its diff:
```python
import functools
import math

import jax
import jax.numpy as jnp
from jax import lax
from jax.experimental import pallas as pl
from jax.experimental.pallas import tpu as pltpu
from jax.sharding import PartitionSpec as P

HEAD = 128
GROUP = 8
WINDOW = 4
MESH = pl.DeviceIdType.MESH


def kernel(n, T, rows, groups, q_hbm, k_hbm, v_hbm, bp, out, qv, kv, bias,
           ld_sem, kv_send, kv_recv, x_send, x_recv, c_send, c_recv):
    s = lax.axis_index("seq")
    t = lax.axis_index("tensor")
    heads = groups * GROUP
    hops = T // 2 - 1
    half = rows // 2

    def seq_dev(d):
        return (lax.rem(s + d + n, n), t)

    def x_dev(k):
        return (s, lax.rem(t + 2 * k + T, T))

    sibling = (s, t + 1 - 2 * lax.rem(t, 2))

    loads = []
    for g in range(groups):
        cols = pl.ds(g * HEAD, HEAD)
        pair = []
        for i, src in enumerate((k_hbm, v_hbm)):
            c = pltpu.make_async_copy(src.at[:, cols], kv.at[g, 0, i], ld_sem.at[g, i])
            c.start()
            pair.append(c)
        loads.append(pair)
    q_load = pltpu.make_async_copy(q_hbm, qv, ld_sem.at[groups, 0])
    q_load.start()

    barrier = pltpu.get_barrier_semaphore()
    peers = [seq_dev(d) for d in (1, 2, 3, -1, -2, -3)] + [sibling]
    peers += [x_dev(k) for k in range(1, hops + 1)]
    for p in peers:
        pl.semaphore_signal(barrier, inc=1, device_id=p, device_id_type=MESH)
    pl.semaphore_wait(barrier, len(peers))

    def kv_copy(g, b):
        return pltpu.make_async_remote_copy(
            src_ref=kv.at[g, 0], dst_ref=kv.at[g, b],
            send_sem=kv_send.at[g, b - 1], recv_sem=kv_recv.at[g, b - 1],
            device_id=seq_dev(b), device_id_type=MESH)

    for g in range(groups):
        for c in loads[g]:
            c.wait()
        for b in (3, 2, 1):
            kv_copy(g, b).start()

    blk = half
    lane = lax.broadcasted_iota(jnp.int32, (blk, blk), 1)
    sub = lax.broadcasted_iota(jnp.int32, (blk, blk), 0)
    for i in range(2):
        qpos = bp[2 * s + i] * blk + sub
        for b in range(WINDOW):
            owner = lax.rem(s - b + n, n)
            for j in range(2):
                kpos = bp[2 * owner + j] * blk + lane
                bias[i * blk:(i + 1) * blk, (2 * b + j) * blk:(2 * b + j + 1) * blk] = (
                    jnp.where(kpos <= qpos, 0.0, -1e30).astype(jnp.float32))
    q_load.wait()

    def piece(owner, h):
        col = pl.multiple_of((owner * heads + h) * HEAD, HEAD)
        return out.at[:, pl.ds(col, HEAD)]

    def x_copy(k, h, owner):
        return pltpu.make_async_remote_copy(
            src_ref=piece(owner, h), dst_ref=piece(owner, h),
            send_sem=x_send.at[k - 1, h], recv_sem=x_recv.at[k - 1, h],
            device_id=x_dev(k), device_id_type=MESH)

    def c_copy(k, h, owner):
        return pltpu.make_async_remote_copy(
            src_ref=piece(owner, h), dst_ref=piece(owner, h),
            send_sem=c_send.at[k, h], recv_sem=c_recv.at[k, h],
            device_id=sibling, device_id_type=MESH)

    factor = math.log2(math.e) / math.sqrt(HEAD)
    window = WINDOW * rows

    for g in range(groups):
        for b in (1, 2, 3):
            kv_copy(g, b).wait_recv()

        def one_head(r, _, g=g):
            h = g * GROUP + r
            qcol = pl.multiple_of(h * HEAD, HEAD)
            ocol = pl.multiple_of((t * heads + h) * HEAD, HEAD)
            keys = kv[g, :, 0].reshape(window, HEAD)
            vals = kv[g, :, 1].reshape(window, HEAD)
            for i in range(2):
                part = slice(i * half, (i + 1) * half)
                q = qv[part, pl.ds(qcol, HEAD)]
                sc = lax.dot_general(q, keys, (((1,), (1,)), ((), ())),
                                     preferred_element_type=jnp.float32)
                sc = sc + bias[part, :]
                top = jnp.max(sc, axis=1, keepdims=True)
                w = jnp.exp2((sc - top) * factor)
                total = jnp.sum(w, axis=1, keepdims=True)
                mixed = jnp.dot(w.astype(jnp.bfloat16), vals,
                                preferred_element_type=jnp.float32)
                out[part, pl.ds(ocol, HEAD)] = (mixed / total).astype(out.dtype)
            for k in range(1, hops + 1):
                x_copy(k, h, t).start()
            c_copy(0, h, t).start()
            return 0

        lax.fori_loop(0, GROUP, one_head, 0)

    def forward(h, _):
        for k in range(1, hops + 1):
            owner = lax.rem(t - 2 * k + T, T)
            x_copy(k, h, owner).wait_recv()
            c_copy(k, h, owner).start()
        return 0

    lax.fori_loop(0, heads, forward, 0)

    def finish(h, _):
        for k in range(hops + 1):
            c_copy(k, h, t).wait()
            if k > 0:
                x_copy(k, h, t).wait_send()
        return 0

    lax.fori_loop(0, heads, finish, 0)
    for g in range(groups):
        for b in (1, 2, 3):
            kv_copy(g, b).wait_send()


def body(n, T, queries, keys, values, block_pos):
    rows = queries.shape[0]
    groups = keys.shape[1] // HEAD
    heads = groups * GROUP
    hops = T // 2 - 1
    dma = pltpu.SemaphoreType.DMA
    return pl.pallas_call(
        functools.partial(kernel, n, T, rows, groups),
        out_shape=jax.ShapeDtypeStruct((rows, queries.shape[1] * T), jnp.bfloat16),
        in_specs=[pl.BlockSpec(memory_space=pltpu.HBM)] * 3
        + [pl.BlockSpec(memory_space=pltpu.SMEM)],
        out_specs=pl.BlockSpec(memory_space=pltpu.VMEM),
        scratch_shapes=[
            pltpu.VMEM((rows, heads * HEAD), jnp.bfloat16),
            pltpu.VMEM((groups, WINDOW, 2, rows, HEAD), jnp.bfloat16),
            pltpu.VMEM((rows, WINDOW * rows), jnp.float32),
            dma((groups + 1, 2)),
            dma((groups, 3)),
            dma((groups, 3)),
            dma((hops, heads)),
            dma((hops, heads)),
            dma((hops + 1, heads)),
            dma((hops + 1, heads)),
        ],
        compiler_params=pltpu.CompilerParams(
            collective_id=0, has_side_effects=True, vmem_limit_bytes=32 * 1024 * 1024),
    )(queries, keys, values, block_pos)


def solution(mesh):
    n, T = mesh.shape["seq"], mesh.shape["tensor"]
    placed = (P("seq", "tensor"), P("seq", "tensor"), P("seq", "tensor"), P())
    return jax.shard_map(functools.partial(body, n, T), mesh=mesh, in_specs=placed,
                         out_specs=P("seq", None), check_vma=False)
```

time: 102 us -> 60.6 us (0.59)
  waiting for transfers between devices: 62.5 us -> 0 us
  Pallas kernels: 0 us -> 54.7 us
  between operations: 13.5 us -> 0.01 us
  other arithmetic: 9.54 us -> 0 us
  matrix products: 6.94 us -> 0 us
  starting transfers between devices: 3.28 us -> 0 us
    pallas_call x0 -> x1, Pallas kernels: none -> 54.7 us  [body(): pl.pallas_call(functools.partial(kernel, n, T, rows, groups), out_shape=j...]
    all_gather x2 -> x0, waiting for transfers between devices: 37 us -> none  [body(): halves.append(lax.all_gather(local, 'tensor', axis=1, tiled=True))]
    ppermute x3 -> x0, waiting for transfers between devices: 25.5 us -> none  [from_behind(): return lax.ppermute(block, axis, route)]
    dot_general x4 -> x0, matrix products: 6.94 us -> none  [the longest x2 4.34 us: attend(): jnp.einsum('grqk,kgd->qgrd', rounded, value_gathered, preferred_element_t...]
    concatenate x2 -> x0, other arithmetic: 4.68 us -> none  [the longest x1 4.67 us: body(): return jnp.concatenate(halves, 0)]
    reduce_sum x2 -> x0, other arithmetic: 3.49 us -> none  [attend(): total = jnp.sum(weights, axis=-1)]
    unnamed x4 -> x9, local copies, waits for them, and re-layouts: 2.55 us -> 5.7 us
    ppermute x3 -> x0, starting transfers between devices: 3.05 us -> none  [from_behind(): return lax.ppermute(block, axis, route)]
  transfers between devices with their start and end apart: 5 -> 0, of which waited for: 5 -> 0; matrix products, arithmetic and copies ran while one was open for 10% -> 0% of each run, Pallas kernels for 0% -> 0%
where the time goes in v1:
time: 60.6 us; the launch traced here: 60.5 us
  Pallas kernels  54.7 us (90%)
  local copies, waits for them, and re-layouts  5.7 us (9%)
    pallas_call x1, Pallas kernels, body(): pl.pallas_call(functools.partial(kernel, n, T, rows, groups), out_shape=j...  54.7 us
    unnamed x9, local copies, waits for them, and re-layouts  5.7 us

profile of v1, /device:TPU:0, one launch (start us, length us, event | category | flops | bytes accessed | tf_op | source)
XLA Modules:
  0.0 60.5 jit_solution(606467946896369774)
XLA Ops:
  0.0 0.0 copy-start
  0.0 1.2 %copy-done = bf16[256,2048]{1,0:T(8,128)(2,1)S(1)} copy-done((bf16[256,2048]{1,0:T(8,128)(2,1)S(1)}, bf16[256,2048]{1,0:T(8,128)(2,1)}, u32[]{:S(2)}) %copy-start) | copy-done | bytes 1048600
  1.2 0.0 copy-start.1
  1.2 0.9 %copy-done.1 = bf16[256,256]{1,0:T(8,128)(2,1)S(1)} copy-done((bf16[256,256]{1,0:T(8,128)(2,1)S(1)}, bf16[256,256]{1,0:T(8,128)(2,1)}, u32[]{:S(2)}) %copy-start.1) | copy-done | bytes 131096
  2.1 0.0 copy-start.2
  2.1 0.9 %copy-done.2 = bf16[256,256]{1,0:T(8,128)(2,1)S(1)} copy-done((bf16[256,256]{1,0:T(8,128)(2,1)S(1)}, bf16[256,256]{1,0:T(8,128)(2,1)}, u32[]{:S(2)}) %copy-start.2) | copy-done | bytes 131096
  3.0 0.0 copy-start.3
  3.0 0.7 %copy-done.3 = s32[16]{0:T(128)S(1)} copy-done((s32[16]{0:T(128)S(1)}, s32[16]{0:T(128)}, u32[]{:S(2)}) %copy-start.3) | copy-done | bytes 88
  3.7 54.7 %shard_map.46 = bf16[256,8192]{1,0:T(8,128)(2,1)S(1)} custom-call(bf16[256,2048]{1,0:T(8,128)(2,1)S(1)} %copy-done, bf16[256,256]{1,0:T(8,128)(2,1)S(1)} %copy-done.1, bf16[256,256]{1,0:T(8,128)(2,1)S(1)} %copy-done.2, s32[16]{0:T(128)S(1)} %copy-done.3), custom_call_target="tpu_custom_call" | custom-call | tf_op jit(solution)/shard_map/pallas_call | solution.py:153
  58.4 2.0 %copy.6 = bf16[256,8192]{1,0:T(8,128)(2,1)} copy(bf16[256,8192]{1,0:T(8,128)(2,1)S(1)} %shard_map.46) | data formatting | bytes 8388608
Async XLA Ops:
  0.0 1.2 %copy-start = (bf16[256,2048]{1,0:T(8,128)(2,1)S(1)}, bf16[256,2048]{1,0:T(8,128)(2,1)}, u32[]{:S(2)}) copy-start(bf16[256,2048]{1,0:T(8,128)(2,1)} %q_hbm.1) | copy-start | bytes 3145732
  1.2 0.9 %copy-start.1 = (bf16[256,256]{1,0:T(8,128)(2,1)S(1)}, bf16[256,256]{1,0:T(8,128)(2,1)}, u32[]{:S(2)}) copy-start(bf16[256,256]{1,0:T(8,128)(2,1)} %k_hbm.1) | copy-start | bytes 393220
  2.1 0.9 %copy-start.2 = (bf16[256,256]{1,0:T(8,128)(2,1)S(1)}, bf16[256,256]{1,0:T(8,128)(2,1)}, u32[]{:S(2)}) copy-start(bf16[256,256]{1,0:T(8,128)(2,1)} %v_hbm.1) | copy-start | bytes 393220
  3.0 0.7 %copy-start.3 = (s32[16]{0:T(128)S(1)}, s32[16]{0:T(128)}, u32[]{:S(2)}) copy-start(s32[16]{0:T(128)} %bp.1) | copy-start | bytes 196

commit v2 on v1

--- a/solution.py
+++ b/solution.py
@@ -14,7 +14,7 @@
 MESH = pl.DeviceIdType.MESH
 
 
-def kernel(n, T, rows, groups, q_hbm, k_hbm, v_hbm, bp, out, qv, kv, bias,
+def kernel(n, T, rows, groups, q_hbm, k_hbm, v_hbm, bp_hbm, out, bp, qv, kv, bias,
            ld_sem, kv_send, kv_recv, x_send, x_recv, c_send, c_recv):
     s = lax.axis_index("seq")
     t = lax.axis_index("tensor")
@@ -41,26 +41,51 @@
         loads.append(pair)
     q_load = pltpu.make_async_copy(q_hbm, qv, ld_sem.at[groups, 0])
     q_load.start()
+    bp_load = pltpu.make_async_copy(bp_hbm, bp, ld_sem.at[groups, 1])
+    bp_load.start()
 
     barrier = pltpu.get_barrier_semaphore()
-    peers = [seq_dev(d) for d in (1, 2, 3, -1, -2, -3)] + [sibling]
+    peers = [seq_dev(d) for d in (1, 2, -1, -2)] + [sibling]
     peers += [x_dev(k) for k in range(1, hops + 1)]
     for p in peers:
         pl.semaphore_signal(barrier, inc=1, device_id=p, device_id_type=MESH)
     pl.semaphore_wait(barrier, len(peers))
 
-    def kv_copy(g, b):
+    odd = lax.rem(s, 2)
+
+    def kv_copy(g, i, b, src, d):
         return pltpu.make_async_remote_copy(
-            src_ref=kv.at[g, 0], dst_ref=kv.at[g, b],
-            send_sem=kv_send.at[g, b - 1], recv_sem=kv_recv.at[g, b - 1],
-            device_id=seq_dev(b), device_id_type=MESH)
-
-    for g in range(groups):
-        for c in loads[g]:
-            c.wait()
-        for b in (3, 2, 1):
-            kv_copy(g, b).start()
-
+            src_ref=kv.at[g, src, i], dst_ref=kv.at[g, b, i],
+            send_sem=kv_send.at[g, i, b - 1], recv_sem=kv_recv.at[g, i, b - 1],
+            device_id=seq_dev(d), device_id_type=MESH)
+
+    def two(g, i):
+        return kv_copy(g, i, 2, 0, 2)
+
+    def three(g, i):
+        return kv_copy(g, i, 3, 2, 1)
+
+    def send_own(g):
+        for i in range(2):
+            loads[g][i].wait()
+            two(g, i).start()
+
+            @pl.when(odd == 0)
+            def _():
+                kv_copy(g, i, 1, 0, 1).start()
+
+    def send_on(g):
+        for i in range(2):
+            two(g, i).wait_recv()
+
+            @pl.when(odd == 1)
+            def _():
+                kv_copy(g, i, 1, 2, -1).start()
+
+            three(g, i).start()
+
+    send_own(0)
+    bp_load.wait()
     blk = half
     lane = lax.broadcasted_iota(jnp.int32, (blk, blk), 1)
     sub = lax.broadcasted_iota(jnp.int32, (blk, blk), 0)
@@ -73,6 +98,9 @@
                 bias[i * blk:(i + 1) * blk, (2 * b + j) * blk:(2 * b + j + 1) * blk] = (
                     jnp.where(kpos <= qpos, 0.0, -1e30).astype(jnp.float32))
     q_load.wait()
+    send_on(0)
+    for g in range(1, groups):
+        send_own(g)
 
     def piece(owner, h):
         col = pl.multiple_of((owner * heads + h) * HEAD, HEAD)
@@ -94,8 +122,9 @@
     window = WINDOW * rows
 
     for g in range(groups):
-        for b in (1, 2, 3):
-            kv_copy(g, b).wait_recv()
+        for i in range(2):
+            kv_copy(g, i, 1, 0, 1).wait_recv()
+            three(g, i).wait_recv()
 
         def one_head(r, _, g=g):
             h = g * GROUP + r
@@ -120,7 +149,10 @@
             c_copy(0, h, t).start()
             return 0
 
-        lax.fori_loop(0, GROUP, one_head, 0)
+        lax.fori_loop(0, GROUP // 2, one_head, 0)
+        if g + 1 < groups:
+            send_on(g + 1)
+        lax.fori_loop(GROUP // 2, GROUP, one_head, 0)
 
     def forward(h, _):
         for k in range(1, hops + 1):
@@ -140,8 +172,10 @@
 
     lax.fori_loop(0, heads, finish, 0)
     for g in range(groups):
-        for b in (1, 2, 3):
-            kv_copy(g, b).wait_send()
+        for i in range(2):
+            kv_copy(g, i, 1, 0, 1).wait_send()
+            two(g, i).wait_send()
+            three(g, i).wait_send()
 
 
 def body(n, T, queries, keys, values, block_pos):
@@ -153,16 +187,16 @@
     return pl.pallas_call(
         functools.partial(kernel, n, T, rows, groups),
         out_shape=jax.ShapeDtypeStruct((rows, queries.shape[1] * T), jnp.bfloat16),
-        in_specs=[pl.BlockSpec(memory_space=pltpu.HBM)] * 3
-        + [pl.BlockSpec(memory_space=pltpu.SMEM)],
+        in_specs=[pl.BlockSpec(memory_space=pltpu.HBM)] * 4,
         out_specs=pl.BlockSpec(memory_space=pltpu.VMEM),
         scratch_shapes=[
+            pltpu.SMEM(block_pos.shape, jnp.int32),
             pltpu.VMEM((rows, heads * HEAD), jnp.bfloat16),
             pltpu.VMEM((groups, WINDOW, 2, rows, HEAD), jnp.bfloat16),
             pltpu.VMEM((rows, WINDOW * rows), jnp.float32),
             dma((groups + 1, 2)),
-            dma((groups, 3)),
-            dma((groups, 3)),
+            dma((groups, 2, 3)),
+            dma((groups, 2, 3)),
             dma((hops, heads)),
             dma((hops, heads)),
             dma((hops + 1, heads)),
@@ -170,7 +204,8 @@
         ],
         compiler_params=pltpu.CompilerParams(
             collective_id=0, has_side_effects=True, vmem_limit_bytes=32 * 1024 * 1024),
-    )(queries, keys, values, block_pos)
+    )(*(pltpu.with_memory_space_constraint(z, pltpu.HBM)
+        for z in (queries, keys, values, block_pos)))
 
 
 def solution(mesh):

time: 60.6 us -> 44.1 us (0.73)
  Pallas kernels: 54.7 us -> 41.9 us
  local copies, waits for them, and re-layouts: 5.7 us -> 2.02 us
    pallas_call x1, Pallas kernels: 54.7 us -> 41.9 us  [body(): pl.pallas_call(functools.partial(kernel, n, T, rows, groups), out_shape=j...]
    unnamed x9 -> x1, local copies, waits for them, and re-layouts: 5.7 us -> 2.02 us
where the time goes in v2:
time: 44.1 us; the launch traced here: 43.9 us
  Pallas kernels  41.9 us (95%)
  local copies, waits for them, and re-layouts  2.02 us (5%)
    pallas_call x1, Pallas kernels, body(): pl.pallas_call(functools.partial(kernel, n, T, rows, groups), out_shape=j...  41.9 us
    unnamed x1, local copies, waits for them, and re-layouts  2.02 us

profile of v2, /device:TPU:0, one launch (start us, length us, event | category | flops | bytes accessed | tf_op | source)
XLA Modules:
  0.0 43.9 jit_solution(18334082894845869169)
XLA Ops:
  0.0 41.9 %shard_map.46 = bf16[256,8192]{1,0:T(8,128)(2,1)S(1)} custom-call(bf16[256,2048]{1,0:T(8,128)(2,1)} %q_hbm.1, bf16[256,256]{1,0:T(8,128)(2,1)} %k_hbm.1, bf16[256,256]{1,0:T(8,128)(2,1)} %v_hbm.1, s32[16]{0:T(128)} %bp_hbm.1), custom_call_target="tpu_custom_call" | custom-call | tf_op jit(solution)/shard_map/pallas_call | solution.py:187
  41.9 2.0 %copy.6 = bf16[256,8192]{1,0:T(8,128)(2,1)} copy(bf16[256,8192]{1,0:T(8,128)(2,1)S(1)} %shard_map.46) | data formatting | bytes 8388608

commit v3 on v2

--- a/solution.py
+++ b/solution.py
@@ -10,6 +10,7 @@
 
 HEAD = 128
 GROUP = 8
+CUTS = 2
 WINDOW = 4
 MESH = pl.DeviceIdType.MESH
 
@@ -53,9 +54,12 @@
 
     odd = lax.rem(s, 2)
 
+    cut = rows // CUTS
+
     def kv_copy(g, i, b, src, d):
+        part = pl.ds(i % CUTS * cut, cut)
         return pltpu.make_async_remote_copy(
-            src_ref=kv.at[g, src, i], dst_ref=kv.at[g, b, i],
+            src_ref=kv.at[g, src, i // CUTS, part], dst_ref=kv.at[g, b, i // CUTS, part],
             send_sem=kv_send.at[g, i, b - 1], recv_sem=kv_recv.at[g, i, b - 1],
             device_id=seq_dev(d), device_id_type=MESH)
 
@@ -66,8 +70,9 @@
         return kv_copy(g, i, 3, 2, 1)
 
     def send_own(g):
-        for i in range(2):
-            loads[g][i].wait()
+        for i in range(2 * CUTS):
+            if i % CUTS == 0:
+                loads[g][i // CUTS].wait()
             two(g, i).start()
 
             @pl.when(odd == 0)
@@ -75,7 +80,7 @@
                 kv_copy(g, i, 1, 0, 1).start()
 
     def send_on(g):
-        for i in range(2):
+        for i in range(2 * CUTS):
             two(g, i).wait_recv()
 
             @pl.when(odd == 1)
@@ -122,7 +127,7 @@
     window = WINDOW * rows
 
     for g in range(groups):
-        for i in range(2):
+        for i in range(2 * CUTS):
             kv_copy(g, i, 1, 0, 1).wait_recv()
             three(g, i).wait_recv()
 
@@ -172,7 +177,7 @@
 
     lax.fori_loop(0, heads, finish, 0)
     for g in range(groups):
-        for i in range(2):
+        for i in range(2 * CUTS):
             kv_copy(g, i, 1, 0, 1).wait_send()
             two(g, i).wait_send()
             three(g, i).wait_send()
@@ -195,8 +200,8 @@
             pltpu.VMEM((groups, WINDOW, 2, rows, HEAD), jnp.bfloat16),
             pltpu.VMEM((rows, WINDOW * rows), jnp.float32),
             dma((groups + 1, 2)),
-            dma((groups, 2, 3)),
-            dma((groups, 2, 3)),
+            dma((groups, 2 * CUTS, 3)),
+            dma((groups, 2 * CUTS, 3)),
             dma((hops, heads)),
             dma((hops, heads)),
             dma((hops + 1, heads)),

time: 44.1 us -> 43.5 us (0.986)
  Pallas kernels: 41.9 us -> 41.3 us
    pallas_call x1, Pallas kernels: 41.9 us -> 41.3 us  [body(): pl.pallas_call(functools.partial(kernel, n, T, rows, groups), out_shape=j...]
where the time goes in v3:
time: 43.5 us; the launch traced here: 43.3 us
  Pallas kernels  41.3 us (95%)
  local copies, waits for them, and re-layouts  2.02 us (5%)
    pallas_call x1, Pallas kernels, body(): pl.pallas_call(functools.partial(kernel, n, T, rows, groups), out_shape=j...  41.3 us
    unnamed x1, local copies, waits for them, and re-layouts  2.02 us

profile of v3, /device:TPU:0, one launch (start us, length us, event | category | flops | bytes accessed | tf_op | source)
XLA Modules:
  0.0 43.3 jit_solution(1256592951564525732)
XLA Ops:
  0.0 41.3 %shard_map.46 = bf16[256,8192]{1,0:T(8,128)(2,1)S(1)} custom-call(bf16[256,2048]{1,0:T(8,128)(2,1)} %q_hbm.1, bf16[256,256]{1,0:T(8,128)(2,1)} %k_hbm.1, bf16[256,256]{1,0:T(8,128)(2,1)} %v_hbm.1, s32[16]{0:T(128)} %bp_hbm.1), custom_call_target="tpu_custom_call" | custom-call | tf_op jit(solution)/shard_map/pallas_call | solution.py:192
  41.3 2.0 %copy.6 = bf16[256,8192]{1,0:T(8,128)(2,1)} copy(bf16[256,8192]{1,0:T(8,128)(2,1)S(1)} %shard_map.46) | data formatting | bytes 8388608

commit v4 on v3

--- a/solution.py
+++ b/solution.py
@@ -127,16 +127,19 @@
     window = WINDOW * rows
 
     for g in range(groups):
-        for i in range(2 * CUTS):
-            kv_copy(g, i, 1, 0, 1).wait_recv()
-            three(g, i).wait_recv()
-
-        def one_head(r, _, g=g):
+        def arrive(which, g=g):
+            for i in range(which * CUTS, (which + 1) * CUTS):
+                kv_copy(g, i, 1, 0, 1).wait_recv()
+                three(g, i).wait_recv()
+
+        arrive(0)
+
+        def one_head(r, _, g=g, late=None):
             h = g * GROUP + r
             qcol = pl.multiple_of(h * HEAD, HEAD)
             ocol = pl.multiple_of((t * heads + h) * HEAD, HEAD)
             keys = kv[g, :, 0].reshape(window, HEAD)
-            vals = kv[g, :, 1].reshape(window, HEAD)
+            made = []
             for i in range(2):
                 part = slice(i * half, (i + 1) * half)
                 q = qv[part, pl.ds(qcol, HEAD)]
@@ -146,15 +149,20 @@
                 top = jnp.max(sc, axis=1, keepdims=True)
                 w = jnp.exp2((sc - top) * factor)
                 total = jnp.sum(w, axis=1, keepdims=True)
-                mixed = jnp.dot(w.astype(jnp.bfloat16), vals,
-                                preferred_element_type=jnp.float32)
+                made.append((part, w.astype(jnp.bfloat16), total))
+            if late is not None:
+                late(1)
+            vals = kv[g, :, 1].reshape(window, HEAD)
+            for part, w, total in made:
+                mixed = jnp.dot(w, vals, preferred_element_type=jnp.float32)
                 out[part, pl.ds(ocol, HEAD)] = (mixed / total).astype(out.dtype)
             for k in range(1, hops + 1):
                 x_copy(k, h, t).start()
             c_copy(0, h, t).start()
             return 0
 
-        lax.fori_loop(0, GROUP // 2, one_head, 0)
+        one_head(0, 0, late=arrive)
+        lax.fori_loop(1, GROUP // 2, one_head, 0)
         if g + 1 < groups:
             send_on(g + 1)
         lax.fori_loop(GROUP // 2, GROUP, one_head, 0)

time: 43.5 us -> 42.4 us (0.975)
  Pallas kernels: 41.3 us -> 40.2 us
    pallas_call x1, Pallas kernels: 41.3 us -> 40.2 us  [body(): pl.pallas_call(functools.partial(kernel, n, T, rows, groups), out_shape=j...]
where the time goes in v4:
time: 42.4 us; the launch traced here: 42.3 us
  Pallas kernels  40.2 us (95%)
  local copies, waits for them, and re-layouts  2.02 us (5%)
    pallas_call x1, Pallas kernels, body(): pl.pallas_call(functools.partial(kernel, n, T, rows, groups), out_shape=j...  40.2 us
    unnamed x1, local copies, waits for them, and re-layouts  2.02 us

profile of v4, /device:TPU:0, one launch (start us, length us, event | category | flops | bytes accessed | tf_op | source)
XLA Modules:
  0.0 42.3 jit_solution(8735007523170996664)
XLA Ops:
  0.0 40.2 %shard_map.46 = bf16[256,8192]{1,0:T(8,128)(2,1)S(1)} custom-call(bf16[256,2048]{1,0:T(8,128)(2,1)} %q_hbm.1, bf16[256,256]{1,0:T(8,128)(2,1)} %k_hbm.1, bf16[256,256]{1,0:T(8,128)(2,1)} %v_hbm.1, s32[16]{0:T(128)} %bp_hbm.1), custom_call_target="tpu_custom_call" | custom-call | tf_op jit(solution)/shard_map/pallas_call | solution.py:200
  40.2 2.0 %copy.6 = bf16[256,8192]{1,0:T(8,128)(2,1)} copy(bf16[256,8192]{1,0:T(8,128)(2,1)S(1)} %shard_map.46) | data formatting | bytes 8388608

commit v5 on v4

--- a/solution.py
+++ b/solution.py
@@ -56,11 +56,11 @@
 
     cut = rows // CUTS
 
-    def kv_copy(g, i, b, src, d):
+    def kv_copy(g, i, b, src, d, sent=None):
         part = pl.ds(i % CUTS * cut, cut)
         return pltpu.make_async_remote_copy(
             src_ref=kv.at[g, src, i // CUTS, part], dst_ref=kv.at[g, b, i // CUTS, part],
-            send_sem=kv_send.at[g, i, b - 1], recv_sem=kv_recv.at[g, i, b - 1],
+            send_sem=kv_send.at[g, i, b - 1 if sent is None else sent], recv_sem=kv_recv.at[g, i, b - 1],
             device_id=seq_dev(d), device_id_type=MESH)
 
     def two(g, i):
@@ -86,8 +86,15 @@
             @pl.when(odd == 1)
             def _():
                 kv_copy(g, i, 1, 2, -1).start()
-
-            three(g, i).start()
+                three(g, i).start()
+                if i % 2:
+                    kv_copy(g, i, 1, 0, 1).wait_recv()
+                    kv_copy(g, i, 3, 1, 2, 3).start()
+
+            if i % 2 == 0:
+                @pl.when(odd == 0)
+                def _():
+                    three(g, i).start()
 
     send_own(0)
     bp_load.wait()
@@ -129,7 +136,12 @@
     for g in range(groups):
         def arrive(which, g=g):
             for i in range(which * CUTS, (which + 1) * CUTS):
-                kv_copy(g, i, 1, 0, 1).wait_recv()
+                if i % 2:
+                    @pl.when(odd == 0)
+                    def _():
+                        kv_copy(g, i, 1, 0, 1).wait_recv()
+                else:
+                    kv_copy(g, i, 1, 0, 1).wait_recv()
                 three(g, i).wait_recv()
 
         arrive(0)
@@ -188,7 +200,13 @@
         for i in range(2 * CUTS):
             kv_copy(g, i, 1, 0, 1).wait_send()
             two(g, i).wait_send()
-            three(g, i).wait_send()
+            if i % 2:
+                @pl.when(odd == 1)
+                def _():
+                    three(g, i).wait_send()
+                    kv_copy(g, i, 3, 1, 2, 3).wait_send()
+            else:
+                three(g, i).wait_send()
 
 
 def body(n, T, queries, keys, values, block_pos):
@@ -208,7 +226,7 @@
             pltpu.VMEM((groups, WINDOW, 2, rows, HEAD), jnp.bfloat16),
             pltpu.VMEM((rows, WINDOW * rows), jnp.float32),
             dma((groups + 1, 2)),
-            dma((groups, 2 * CUTS, 3)),
+            dma((groups, 2 * CUTS, 4)),
             dma((groups, 2 * CUTS, 3)),
             dma((hops, heads)),
             dma((hops, heads)),

time: 42.4 us -> 42.4 us (level)
  no operation moved by 1% of the time
where the time goes in v5:
time: 42.4 us; the launch traced here: 42.2 us
  Pallas kernels  40.2 us (95%)
  local copies, waits for them, and re-layouts  2.02 us (5%)
    pallas_call x1, Pallas kernels, body(): pl.pallas_call(functools.partial(kernel, n, T, rows, groups), out_shape=j...  40.2 us
    unnamed x1, local copies, waits for them, and re-layouts  2.02 us

profile of v5, /device:TPU:0, one launch (start us, length us, event | category | flops | bytes accessed | tf_op | source)
XLA Modules:
  0.0 42.2 jit_solution(10212876147238553132)
XLA Ops:
  0.0 40.2 %shard_map.46 = bf16[256,8192]{1,0:T(8,128)(2,1)S(1)} custom-call(bf16[256,2048]{1,0:T(8,128)(2,1)} %q_hbm.1, bf16[256,256]{1,0:T(8,128)(2,1)} %k_hbm.1, bf16[256,256]{1,0:T(8,128)(2,1)} %v_hbm.1, s32[16]{0:T(128)} %bp_hbm.1), custom_call_target="tpu_custom_call" | custom-call | tf_op jit(solution)/shard_map/pallas_call | solution.py:218
  40.2 2.0 %copy.6 = bf16[256,8192]{1,0:T(8,128)(2,1)} copy(bf16[256,8192]{1,0:T(8,128)(2,1)S(1)} %shard_map.46) | data formatting | bytes 8388608
